TPU v7x, 128 devices: a whole 4x4x4 slice. The times are simulated.
128 devices in a mesh: row: 8 (over x_hi, z), col: 16 (over x_lo, y, core).
Axes of the slice: x: 4 (x_hi: 2, x_lo: 2; x = x_hi * 2 + x_lo), y: 4, z: 4, core: 2. Of those that a mesh axis runs over, the one named last changes fastest.
Arguments:
- customer_inputs: bfloat16 [131072, 1024], P(('row', 'col')), may hold values from -6 to 6
- candidate_inputs: bfloat16 [131072, 1024], P(('row', 'col')), may hold values from -6 to 6
- affinity_sharpness: bfloat16 [131072], P(('row', 'col')), may hold values from 4 to 40
- correct_candidate_index: int32 [131072], P(('row', 'col')), may hold values from 0 to 8191
- customer_initial_weights: bfloat16 [1024, 512], replicated, may hold values from -0.1875 to 0.1875
- customer_final_weights: bfloat16 [512, 256], replicated, may hold values from -0.25 to 0.25
- candidate_initial_weights: bfloat16 [1024, 512], replicated, may hold values from -0.1875 to 0.1875
- candidate_final_weights: bfloat16 [512, 256], replicated, may hold values from -0.25 to 0.25
Outputs:
- loss: float32 [], replicated
- grad_user_first: float32 [1024, 512], replicated
- grad_user_second: float32 [512, 256], replicated
- grad_item_first: float32 [1024, 512], replicated
- grad_item_second: float32 [512, 256], replicated
Inputs may be any that keep to these rules, and one draw needn't show every extreme that they name: correct_candidate_index[u] indexes the items of u's group in the order of the steps.
All inputs are finite; a program needn't handle non-finite values.
Results may differ from a plain program's by a relative error of at most 0.015.
Values may be sent and summed in bfloat16 or wider, within the bound.
No kernel may reach another device: no remote copies, remote signals or barrier semaphores. Data moves between devices by JAX's collectives and lax.ppermute only.
A program may use at most 128 MiB of HBM per device.

v0:
```python
import jax
import jax.numpy as jnp
from jax import lax
from jax.sharding import PartitionSpec as P

EPS = 1e-06


def laid_out(tiles, dim):
    dims = list(tiles.shape[1:])
    dims[dim] *= tiles.shape[0]
    return jnp.moveaxis(tiles, 0, dim).reshape(dims)


def copy_for_each(value, axis):
    copies = jnp.broadcast_to(value, (lax.axis_size(axis), *value.shape))
    return lax.all_to_all(copies, axis, split_axis=0, concat_axis=0, tiled=True)


def gathered_copies(value, axis, dim):
    return laid_out(copy_for_each(value, axis), dim)


def tower_forward(feats, first, second):
    pre = jnp.dot(feats, first, preferred_element_type=jnp.float32)
    hidden = jax.nn.relu(pre).astype(jnp.bfloat16)
    out = jnp.dot(hidden, second, preferred_element_type=jnp.float32)
    inv = lax.rsqrt(jnp.mean(out * out, axis=-1, keepdims=True) + EPS)
    return ((out * inv).astype(jnp.bfloat16), (pre, hidden, out, inv))


def tower_backward(feats, second, saved, grad_vec):
    pre, hidden, out, inv = saved
    grad = grad_vec.astype(jnp.float32)
    normed = out * inv
    grad_out = (inv * (grad - normed * jnp.mean(grad * normed, axis=-1, keepdims=True))).astype(
        jnp.bfloat16
    )
    grad_second = jnp.dot(hidden.T, grad_out, preferred_element_type=jnp.float32)
    grad_hidden = jnp.dot(grad_out, second.T, preferred_element_type=jnp.float32)
    grad_pre = jnp.where(pre > 0, grad_hidden, 0.0).astype(jnp.bfloat16)
    grad_first = jnp.dot(feats.T, grad_pre, preferred_element_type=jnp.float32)
    return (grad_first, grad_second)


def positive_pair_logit(
    shopper_vector, gathered_entries, affinity_sharpness, correct_candidate_index, resident_table
):
    latent_code = shopper_vector.shape[-1]
    coolness_fp32_number = affinity_sharpness.astype(jnp.float32)
    affinity_matrix = (
        coolness_fp32_number[:, None]
        * jnp.einsum(
            "ue,ie->ui", shopper_vector, gathered_entries, preferred_element_type=jnp.float32
        )
        / latent_code
    )
    lse = jax.nn.logsumexp(affinity_matrix, axis=1)
    columns = lax.broadcasted_iota(jnp.int32, affinity_matrix.shape, 1)
    target_column = columns == correct_candidate_index[:, None]
    picked = jnp.sum(jnp.where(target_column, affinity_matrix, 0.0), axis=1)
    softmax_likelihood = jnp.exp(affinity_matrix - lse[:, None])
    sensitivity_of_affinities = (
        (softmax_likelihood - target_column.astype(jnp.float32))
        * (coolness_fp32_number / (latent_code * resident_table))[:, None]
    ).astype(jnp.bfloat16)
    customer_derivative = jnp.dot(
        sensitivity_of_affinities, gathered_entries, preferred_element_type=jnp.float32
    )
    return (lse, sensitivity_of_affinities, customer_derivative, jnp.sum(lse - picked))


def body(
    customer_inputs,
    candidate_inputs,
    affinity_sharpness,
    correct_candidate_index,
    customer_initial_weights,
    customer_final_weights,
    candidate_initial_weights,
    candidate_final_weights,
):
    resident_table = customer_inputs.shape[0]
    shopper_vector, user_saved = tower_forward(
        customer_inputs, customer_initial_weights, customer_final_weights
    )
    offered_thing_vector, item_saved = tower_forward(
        candidate_inputs, candidate_initial_weights, candidate_final_weights
    )
    latent_code = shopper_vector.shape[-1]
    gathered_entries = lax.all_gather(offered_thing_vector, "row", axis=0, tiled=True)
    lse, sensitivity_of_affinities, customer_derivative, loss_local = positive_pair_logit(
        shopper_vector,
        gathered_entries,
        affinity_sharpness,
        correct_candidate_index,
        resident_table,
    )
    all_users, all_scales = (
        lax.all_gather(shopper_vector, "row", axis=0, tiled=True),
        lax.all_gather(affinity_sharpness, "row", axis=0, tiled=True),
    )
    all_positive = gathered_copies(correct_candidate_index, "row", 0)
    all_lse = gathered_copies(lse, "row", 0)
    coolness_fp32_number = all_scales.astype(jnp.float32)
    affinity_matrix = (
        coolness_fp32_number[:, None]
        * jnp.einsum(
            "ue,ie->ui", all_users, offered_thing_vector, preferred_element_type=jnp.float32
        )
        / latent_code
    )
    start = lax.axis_index("row") * resident_table
    columns = lax.broadcasted_iota(jnp.int32, affinity_matrix.shape, 1) + start
    target_column = columns == all_positive[:, None]
    softmax_likelihood = jnp.exp(affinity_matrix - all_lse[:, None])
    group_dlogits = (
        (softmax_likelihood - target_column.astype(jnp.float32))
        * (coolness_fp32_number / (latent_code * resident_table))[:, None]
    ).astype(jnp.bfloat16)
    candidate_derivative = jnp.einsum(
        "ui,ue->ie", group_dlogits, all_users, preferred_element_type=jnp.float32
    )
    grad_user_first, grad_user_second = tower_backward(
        customer_inputs,
        customer_final_weights,
        user_saved,
        customer_derivative.astype(jnp.bfloat16),
    )
    grad_item_first, grad_item_second = tower_backward(
        candidate_inputs,
        candidate_final_weights,
        item_saved,
        candidate_derivative.astype(jnp.bfloat16),
    )
    summed = (
        lax.psum(grad_user_first.astype(jnp.bfloat16), ("row", "col")).astype(jnp.float32),
        lax.psum(grad_user_second.astype(jnp.bfloat16), ("row", "col")).astype(jnp.float32),
        lax.psum(grad_item_first.astype(jnp.bfloat16), ("row", "col")).astype(jnp.float32),
        lax.psum(grad_item_second.astype(jnp.bfloat16), ("row", "col")).astype(jnp.float32),
        lax.psum(loss_local.astype(jnp.bfloat16), ("row", "col")).astype(jnp.float32),
    )
    users_total = resident_table * lax.axis_size("row") * lax.axis_size("col")
    return (summed[4] / users_total, summed[0], summed[1], summed[2], summed[3])


def solution(mesh):
    placed = (
        P(("row", "col"), None),
        P(("row", "col"), None),
        P(("row", "col")),
        P(("row", "col")),
        P(),
        P(),
        P(),
        P(),
    )
    return jax.shard_map(
        body, mesh=mesh, in_specs=placed, out_specs=(P(), P(), P(), P(), P()), check_vma=False
    )
```

profile of v0, /device:TPU:1, one launch (start us, length us, event | category | flops | bytes accessed | tf_op | source)
XLA Modules:
  0.0 351.3 jit_solution(15818196188370760790)
XLA Ops:
  7.2 0.0 copy-start
  7.2 0.0 copy-start.11
  7.2 0.0 all-gather.3.cloned.1.call-start
  7.2 3.3 fusion.28
  10.5 0.0 copy-start.4
  10.5 1.3 copy-done.4
  11.8 0.5 multiply_reduce_fusion
  12.4 0.9 multiply_convert_fusion.8
  13.3 0.0 all-gather.3.cloned.1.call-update
  13.3 0.6 broadcast_in_dim.15
  13.9 8.3 %all-to-all-start.1 = ((s32[8,1,1024]{2,1,0:T(1,128)}), s32[8,1,1024]{2,1,0:T(1,128)S(1)}, u32[]{:S(2)}, u32[]{:S(2)}) async-start(s32[8,1,1024]{2,1,0:T(1,128)} %broadcast_in_dim.15), calls=%async_computation.1 | async-start | bytes 65536 | tf_op jit(solution)/shard_map/all_to_all | solution.py:17
  22.2 0.0 all-gather.5.cloned.1.call-start
  22.3 2.5 fusion.27
  24.8 0.0 copy-start.6
  24.8 1.3 copy-done.6
  26.1 0.5 multiply_reduce_fusion.1
  26.7 0.9 copy-done.2
  27.6 0.9 multiply_convert_fusion.9
  28.5 0.0 all-gather.5.cloned.1.call-update
  28.6 26.5 %all_gather.10 = bf16[8192]{0:T(1024)(128)(2,1)S(1)} all-gather(bf16[1024]{0:T(1024)(128)(2,1)S(1)} %copy-done.13), channel_id=1, replica_groups=mesh['row'=8,'col'=16] {'row'}, dimensions={0}, use_global_device_ids=true | all-gather | bytes 18432 | tf_op jit(solution)/shard_map/all_gather | solution.py:101
  55.1 32.1 %all-gather.3.cloned.1.call-done = bf16[8192,256]{0,1:T(8,128)(2,1)} async-done(((bf16[1024,256]{0,1:T(8,128)(2,1)}), bf16[8192,256]{0,1:T(8,128)(2,1)}) %all-gather.3.cloned.1.call-update) | async-done | bytes 4194320 | tf_op jit(solution)/shard_map/all_gather | solution.py:91
  87.2 16.0 %fusion = (f32[1024]{0:T(1024)S(1)}, f32[1024,8192]{1,0:T(8,128)}) fusion(f32[1024]{0:T(1024)S(1)} %convert_element_type.90, bf16[1024,256]{0,1:T(8,128)(2,1)} %multiply_convert_fusion.9, bf16[8192,256]{0,1:T(8,128)(2,1)} %all-gather.3.cloned.1.call-done), kind=kOutput, calls=%fused_computation.6 | convolution fusion | flops 4320132096 | bytes 38281216 | tf_op jit(solution)/shard_map/ue,ie->ui/dot_general | solution.py:53
  103.2 18.4 %select_reduce_fusion = (f32[1024]{0:T(1024)S(1)}, f32[1024]{0:T(1024)S(1)}) fusion(f32[1024,8192]{1,0:T(8,128)} %get-tuple-element.28, s32[1024]{0:T(1024)S(1)} %copy-done.14, f32[1024]{0:T(1024)S(1)} %convert_element_type.90, f32[1024]{0:T(1024)S(1)} %is-finite_select_fusion), kind=kLoop, calls=%fused_computation.2 | loop fusion | flops 58718208 | bytes 33574912 | tf_op jit(solution)/shard_map/reduce_sum | solution.py:61
  121.6 0.6 subtract_reduce_fusion
  122.3 20.4 %fusion.9 = (f32[1024]{0:T(1024)S(1)}, bf16[1024,256]{0,1:T(8,128)(2,1)S(1)}) fusion(f32[1024,256]{0,1:T(8,128)S(1)} %copy-done.3, f32[1024]{0:T(1024)S(1)} %add_rsqrt_fusion.1, bf16[8192,256]{0,1:T(8,128)(2,1)} %all-gather.3.cloned.1.call-done, f32[1024,8192]{1,0:T(8,128)} %get-tuple-element.28, f32[1024]{0:T(1024)S(1)} %broadcast_multiply_fusion.1, ...), kind=kOutput, calls=%fused_computation.26 | convolution fusion | flops 4363385856 | bytes 39346176 | tf_op jit(solution)/shard_map/dot_general | solution.py:67
  142.6 1.0 fusion.11
  143.6 4.4 %fusion.5 = bf16[1024,512]{0,1:T(8,128)(2,1)} fusion(bf16[1024,1024]{1,0:T(8,128)(2,1)S(1)} %copy-done, f32[1024,512]{1,0:T(8,128)} %copy-done.6, bf16[1024,256]{0,1:T(8,128)(2,1)} %fusion.11, bf16[512,256]{1,0:T(8,128)(2,1)S(1)} %copy-done.10), kind=kOutput, calls=%fused_computation.16 | convolution fusion | flops 1344274432 | bytes 6029312 | tf_op jit(solution)/shard_map/dot_general | solution.py:42
  148.0 0.6 broadcast_in_dim.14
  148.6 3.3 all-to-all-start
  152.0 0.0 all-reduce.3.cloned.1.call-start
  152.0 2.9 convolution_convert_fusion.3
  154.9 4.5 %all-gather.5.cloned.1.call-done = bf16[8192,256]{0,1:T(8,128)(2,1)} async-done(((bf16[1024,256]{0,1:T(8,128)(2,1)}), bf16[8192,256]{0,1:T(8,128)(2,1)}) %all-gather.5.cloned.1.call-update) | async-done | bytes 4194320 | tf_op jit(solution)/shard_map/all_gather | solution.py:100
  159.4 0.0 all-to-all-done
  159.4 14.2 %multiply_convert_fusion.5.clone.4 = bf16[8192,1024]{1,0:T(8,128)(2,1)S(1)} fusion(f32[8192]{0:T(1024)S(1)} %broadcast_multiply_fusion, s32[1024]{0:T(1024)S(1)} %iota_add_fusion, f32[8192]{0:T(1024)S(1)} %bitcast.31, f32[8192]{0:T(1024)S(1)} %convert_element_type.108, s32[8192]{0:T(1024)S(1)} %bitcast.30, ...), kind=kOutput, calls=%fused_computation.clone.clone.clone.clone.clone.clone.1 | convolution fusion | flops 4362600448 | bytes 22159360 | tf_op jit(solution)/shard_map/ue,ie->ui/dot_general | solution.py:108
  173.6 0.0 copy-start.5
  173.6 0.0 copy-start.12
  173.7 4.7 %fusion.12 = (f32[1024]{0:T(1024)S(1)}, bf16[1024,256]{0,1:T(8,128)(2,1)S(1)}) fusion(f32[1024,256]{0,1:T(8,128)S(1)} %get-tuple-element.26, f32[1024]{0:T(1024)S(1)} %add_rsqrt_fusion, bf16[8192,256]{0,1:T(8,128)(2,1)S(1)} %copy-done.15, bf16[8192,1024]{1,0:T(8,128)(2,1)S(1)} %multiply_convert_fusion.5.clone.4), kind=kOutput, calls=%fused_computation.29 | convolution fusion | flops 4296276992 | bytes 22552576 | tf_op jit(solution)/shard_map/ui,ue->ie/dot_general | solution.py:121
  178.3 1.0 fusion.14
  179.3 4.4 %fusion.6 = bf16[1024,512]{0,1:T(8,128)(2,1)} fusion(bf16[1024,1024]{1,0:T(8,128)(2,1)} %param.9, f32[1024,512]{1,0:T(8,128)S(1)} %copy-done.5, bf16[1024,256]{0,1:T(8,128)(2,1)} %fusion.14, bf16[512,256]{1,0:T(8,128)(2,1)S(1)} %copy-done.12), kind=kOutput, calls=%fused_computation.17 | convolution fusion | flops 1344274432 | bytes 6029312 | tf_op jit(solution)/shard_map/dot_general | solution.py:42
  183.7 1.2 convolution_convert_fusion.2
  184.9 0.0 all-reduce.3.cloned.1.call-update
  185.0 0.0 copy-start.1
  185.0 64.6 %psum.35 = bf16[]{:T(256)} all-reduce(bf16[]{:T(256)} %get-tuple-element.21), channel_id=1, replica_groups=mesh['row'=8,'col'=16] {'row','col'}, use_global_device_ids=true, to_apply=%region_6.7 | all-reduce | flops 1 | bytes 4 | tf_op jit(solution)/shard_map/psum | solution.py:141
  250.2 86.5 %all-reduce.3.cloned.1.call-done = (bf16[1024,512]{0,1:T(8,128)(2,1)}, bf16[1024,512]{0,1:T(8,128)(2,1)}, bf16[512,256]{1,0:T(8,128)(2,1)}, bf16[512,256]{1,0:T(8,128)(2,1)}) async-done(((bf16[1024,512]{0,1:T(8,128)(2,1)}, bf16[1024,512]{0,1:T(8,128)(2,1)}, bf16[512,256]{1,0:T(8,128)(2,1)}, bf16[512,256]{1,0:T(8,128)(2,1)}), (bf16[1024,512]{0,1:T(8,128)(2,1)}, bf16[1024,512]{0,1:T(8,128)(2,1)}, ...) | async-done | bytes 2621456 | tf_op jit(solution)/shard_map/psum | solution.py:137
  336.8 2.7 copy.15
  339.5 1.8 convert_element_type.107
  341.2 1.6 copy.16
  342.8 0.8 convert_element_type.119
  (33 shorter events, 0.1 us)
Async XLA Ops:
  7.2 15.1 %copy-start = (bf16[1024,1024]{1,0:T(8,128)(2,1)S(1)}, bf16[1024,1024]{1,0:T(8,128)(2,1)}, u32[]{:S(2)}) copy-start(bf16[1024,1024]{1,0:T(8,128)(2,1)} %param.8) | copy-start | bytes 6291460
  7.2 4.7 %copy-start.11 = (bf16[512,256]{1,0:T(8,128)(2,1)S(1)}, bf16[512,256]{1,0:T(8,128)(2,1)}, u32[]{:S(2)}) copy-start(bf16[512,256]{1,0:T(8,128)(2,1)} %param.15) | copy-start | bytes 786436
  7.2 80.0 %all-gather.3.cloned.1.call-start = ((), (), s32[]{:S(2)}) async-start(), calls=%async_computation.2 | async-start | bytes 4718592 | tf_op jit(solution)/shard_map/all_gather | solution.py:91
  10.5 1.3 copy-start.4
  11.8 1.4 copy-start.14
  13.9 134.1 %all-to-all-start.1 = ((s32[8,1,1024]{2,1,0:T(1,128)}), s32[8,1,1024]{2,1,0:T(1,128)S(1)}, u32[]{:S(2)}, u32[]{:S(2)}) async-start(s32[8,1,1024]{2,1,0:T(1,128)} %broadcast_in_dim.15), calls=%async_computation.1 | async-start | bytes 65536 | tf_op jit(solution)/shard_map/all_to_all | solution.py:17
  22.2 3.9 %copy-start.10 = (bf16[512,256]{1,0:T(8,128)(2,1)S(1)}, bf16[512,256]{1,0:T(8,128)(2,1)}, u32[]{:S(2)}) copy-start(bf16[512,256]{1,0:T(8,128)(2,1)} %param.13) | copy-start | bytes 786436
  22.2 137.2 %all-gather.5.cloned.1.call-start = ((), (), s32[]{:S(2)}) async-start(), calls=%async_computation.3 | async-start | bytes 4718592 | tf_op jit(solution)/shard_map/all_gather | solution.py:100
  24.8 1.3 copy-start.6
  26.1 2.4 copy-start.13
  26.6 1.0 copy-start.2
  103.2 19.0 %copy-start.3 = (f32[1024,256]{0,1:T(8,128)S(1)}, f32[1024,256]{0,1:T(8,128)}, u32[]{:S(2)}) copy-start(f32[1024,256]{0,1:T(8,128)} %copy-done.2) | copy-start | bytes 3145732
  148.6 10.8 %all-to-all-start = ((f32[8,1,1024]{2,1,0:T(1,128)}), f32[8,1,1024]{2,1,0:T(1,128)S(1)}, u32[]{:S(2)}, u32[]{:S(2)}) async-start(f32[8,1,1024]{2,1,0:T(1,128)} %broadcast_in_dim.14), calls=%async_computation | async-start | bytes 65536 | tf_op jit(solution)/shard_map/all_to_all | solution.py:17
  152.0 184.8 %all-reduce.3.cloned.1.call-start = ((), (), s32[]{:S(2)}) async-start(), calls=%async_computation.4 | async-start | bytes 5242880 | tf_op jit(solution)/shard_map/psum | solution.py:137
  159.4 14.2 %copy-start.15 = (bf16[8192,256]{0,1:T(8,128)(2,1)S(1)}, bf16[8192,256]{0,1:T(8,128)(2,1)}, u32[]{:S(2)}) copy-start(bf16[8192,256]{0,1:T(8,128)(2,1)} %all-gather.5.cloned.1.call-done) | copy-start | bytes 12582916
  173.6 5.7 %copy-start.5 = (f32[1024,512]{1,0:T(8,128)S(1)}, f32[1024,512]{1,0:T(8,128)}, u32[]{:S(2)}) copy-start(f32[1024,512]{1,0:T(8,128)} %copy-done.4) | copy-start | bytes 6291460
  173.6 5.7 %copy-start.12 = (bf16[512,256]{1,0:T(8,128)(2,1)S(1)}, bf16[512,256]{1,0:T(8,128)(2,1)}, u32[]{:S(2)}) copy-start(bf16[512,256]{1,0:T(8,128)(2,1)} %param.15) | copy-start | bytes 786436
  179.3 4.4 %copy-start.7 = (bf16[1024,256]{0,1:T(8,128)(2,1)S(1)}, bf16[1024,256]{0,1:T(8,128)(2,1)}, u32[]{:S(2)}) copy-start(bf16[1024,256]{0,1:T(8,128)(2,1)} %fusion.14) | copy-start | bytes 1572868
  185.0 158.7 %copy-start.1 = (bf16[1024,1024]{1,0:T(8,128)(2,1)S(1)}, bf16[1024,1024]{1,0:T(8,128)(2,1)}, u32[]{:S(2)}) copy-start(bf16[1024,1024]{1,0:T(8,128)(2,1)} %param.8) | copy-start | bytes 6291460
  336.8 4.5 %copy-start.8 = (bf16[1024,512]{0,1:T(8,128)(2,1)S(1)}, bf16[1024,512]{0,1:T(8,128)(2,1)}, u32[]{:S(2)}) copy-start(bf16[1024,512]{0,1:T(8,128)(2,1)} %get-tuple-element.18) | copy-start | bytes 3145732
  336.8 6.1 %copy-start.9 = (bf16[512,256]{1,0:T(8,128)(2,1)S(1)}, bf16[512,256]{1,0:T(8,128)(2,1)}, u32[]{:S(2)}) copy-start(bf16[512,256]{1,0:T(8,128)(2,1)} %get-tuple-element.20) | copy-start | bytes 786436
Sparse Core Ops, SparseCore 0:
  13.4 73.7 all-gather.2
  90.1 69.2 all-gather.4
  185.1 151.6 all-reduce.2
where the time goes:
time: 352 us; the launch traced here: 351 us
  waiting for transfers between devices  123 us (35%)
  blocking collectives  91.1 us (26%)
  matrix products  74.8 us (21%)
  other arithmetic  25.5 us (7%)
  between operations  15.8 us (4%)
  starting transfers between devices  11.8 us (3%)
  local copies, waits for them, and re-layouts  9.18 us (3%)
    psum x1, waiting for transfers between devices, body(): lax.psum(grad_user_first.astype(jnp.bfloat16), ('row', 'col'))  86.5 us
    psum x1, blocking collectives, body(): lax.psum(loss_local.astype(jnp.bfloat16), ('row', 'col'))  64.6 us
    all_gather x1, waiting for transfers between devices, body(): lax.all_gather(offered_thing_vector, 'row', axis=0, tiled=True)  32.1 us
    all_gather x1, blocking collectives, body(): lax.all_gather(affinity_sharpness, 'row', axis=0, tiled=True)  26.5 us
    dot_general x1, matrix products, positive_pair_logit(): jnp.dot(sensitivity_of_affinities, gathered_entries, preferred_element_ty...  20.4 us
    reduce_sum x1, other arithmetic, positive_pair_logit(): picked = jnp.sum(jnp.where(target_column, affinity_matrix, 0.0), axis=1)  18.4 us
    dot_general x1, matrix products, positive_pair_logit(): jnp.einsum('ue,ie->ui', shopper_vector, gathered_entries, preferred_eleme...  16 us
    dot_general x1, matrix products, body(): jnp.einsum('ue,ie->ui', all_users, offered_thing_vector, preferred_elemen...  14.2 us
  transfers between devices with their start and end apart: 5, of which 3 were waited for; matrix products, arithmetic and copies ran while one was open for 20% of the time, Pallas kernels for 0%

commit v1 on v0

--- a/solution.py
+++ b/solution.py
@@ -4,6 +4,11 @@
 from jax.sharding import PartitionSpec as P
 
 EPS = 1e-06
+
+
+def axis_by_axis(value_2, inner_axis, outer_axis):
+    inner = lax.psum(value_2, inner_axis)
+    return lax.psum(inner, outer_axis)
 
 
 def laid_out(tiles, dim):
@@ -134,7 +139,7 @@
         candidate_derivative.astype(jnp.bfloat16),
     )
     summed = (
-        lax.psum(grad_user_first.astype(jnp.bfloat16), ("row", "col")).astype(jnp.float32),
+        axis_by_axis(grad_user_first.astype(jnp.bfloat16), "col", "row").astype(jnp.float32),
         lax.psum(grad_user_second.astype(jnp.bfloat16), ("row", "col")).astype(jnp.float32),
         lax.psum(grad_item_first.astype(jnp.bfloat16), ("row", "col")).astype(jnp.float32),
         lax.psum(grad_item_second.astype(jnp.bfloat16), ("row", "col")).astype(jnp.float32),

time: 352 us -> 537 us (1.53)
  waiting for transfers between devices: 123 us -> 298 us
    psum x1 -> x3, waiting for transfers between devices: 86.5 us -> 261 us  [the longest x1 95.5 us: axis_by_axis(): inner = lax.psum(value_2, inner_axis)]
  transfers between devices with their start and end apart: 5 -> 7, of which waited for: 3 -> 5; matrix products, arithmetic and copies ran while one was open for 20% -> 19% of each run, Pallas kernels for 0% -> 0%
where the time goes in v1:
time: 537 us; the launch traced here: 531 us
  waiting for transfers between devices  298 us (55%)
  blocking collectives  94.4 us (18%)
  matrix products  74.8 us (14%)
  other arithmetic  25.6 us (5%)
  between operations  15.8 us (3%)
  starting transfers between devices  11.8 us (2%)
  local copies, waits for them, and re-layouts  10.8 us (2%)
    psum x1, waiting for transfers between devices, axis_by_axis(): inner = lax.psum(value_2, inner_axis)  95.5 us
    psum x1, waiting for transfers between devices, body(): lax.psum(grad_item_first.astype(jnp.bfloat16), ('row', 'col'))  88.4 us
    psum x1, waiting for transfers between devices, axis_by_axis(): return lax.psum(inner, outer_axis)  77.3 us
    psum x1, blocking collectives, body(): lax.psum(loss_local.astype(jnp.bfloat16), ('row', 'col'))  67.8 us
    all_gather x1, waiting for transfers between devices, body(): lax.all_gather(offered_thing_vector, 'row', axis=0, tiled=True)  32.1 us
    all_gather x1, blocking collectives, body(): lax.all_gather(affinity_sharpness, 'row', axis=0, tiled=True)  26.5 us
    dot_general x1, matrix products, positive_pair_logit(): jnp.dot(sensitivity_of_affinities, gathered_entries, preferred_element_ty...  20.4 us
    reduce_sum x1, other arithmetic, positive_pair_logit(): picked = jnp.sum(jnp.where(target_column, affinity_matrix, 0.0), axis=1)  18.4 us
  transfers between devices with their start and end apart: 7, of which 5 were waited for; matrix products, arithmetic and copies ran while one was open for 19% of the time, Pallas kernels for 0%

profile of v1, /device:TPU:1, one launch (start us, length us, event | category | flops | bytes accessed | tf_op | source)
XLA Modules:
  0.0 531.0 jit_solution(14344625796249512213)
XLA Ops:
  7.2 0.0 copy-start
  7.2 0.0 all-gather.3.cloned.1.call-start
  7.2 3.3 fusion.28
  10.5 1.3 copy-done.4
  11.8 0.5 multiply_reduce_fusion
  12.4 0.9 multiply_convert_fusion.8
  13.3 0.0 all-gather.3.cloned.1.call-update
  13.3 0.6 broadcast_in_dim.15
  13.9 8.3 %all-to-all-start.1 = ((s32[8,1,1024]{2,1,0:T(1,128)}), s32[8,1,1024]{2,1,0:T(1,128)S(1)}, u32[]{:S(2)}, u32[]{:S(2)}) async-start(s32[8,1,1024]{2,1,0:T(1,128)} %broadcast_in_dim.15), calls=%async_computation.1 | async-start | bytes 65536 | tf_op jit(solution)/shard_map/all_to_all | solution.py:22
  22.2 0.0 all-gather.5.cloned.1.call-start
  22.3 2.5 fusion.27
  24.8 1.3 copy-done.6
  26.1 0.5 multiply_reduce_fusion.1
  26.7 0.9 copy-done.2
  27.6 0.9 multiply_convert_fusion.9
  28.5 0.0 all-gather.5.cloned.1.call-update
  28.5 26.5 %all_gather.10 = bf16[8192]{0:T(1024)(128)(2,1)S(1)} all-gather(bf16[1024]{0:T(1024)(128)(2,1)S(1)} %copy-done.11), channel_id=1, replica_groups=mesh['row'=8,'col'=16] {'row'}, dimensions={0}, use_global_device_ids=true | all-gather | bytes 18432 | tf_op jit(solution)/shard_map/all_gather | solution.py:106
  55.1 32.1 %all-gather.3.cloned.1.call-done = bf16[8192,256]{0,1:T(8,128)(2,1)} async-done(((bf16[1024,256]{0,1:T(8,128)(2,1)}), bf16[8192,256]{0,1:T(8,128)(2,1)}) %all-gather.3.cloned.1.call-update) | async-done | bytes 4194320 | tf_op jit(solution)/shard_map/all_gather | solution.py:96
  87.2 16.0 %fusion = (f32[1024]{0:T(1024)S(1)}, f32[1024,8192]{1,0:T(8,128)}) fusion(f32[1024]{0:T(1024)S(1)} %convert_element_type.90, bf16[1024,256]{0,1:T(8,128)(2,1)} %multiply_convert_fusion.9, bf16[8192,256]{0,1:T(8,128)(2,1)} %all-gather.3.cloned.1.call-done), kind=kOutput, calls=%fused_computation.6 | convolution fusion | flops 4320132096 | bytes 38281216 | tf_op jit(solution)/shard_map/ue,ie->ui/dot_general | solution.py:58
  103.2 18.4 %select_reduce_fusion = (f32[1024]{0:T(1024)S(1)}, f32[1024]{0:T(1024)S(1)}) fusion(f32[1024,8192]{1,0:T(8,128)} %get-tuple-element.27, s32[1024]{0:T(1024)S(1)} %copy-done.12, f32[1024]{0:T(1024)S(1)} %convert_element_type.90, f32[1024]{0:T(1024)S(1)} %is-finite_select_fusion), kind=kLoop, calls=%fused_computation.2 | loop fusion | flops 58718208 | bytes 33574912 | tf_op jit(solution)/shard_map/reduce_sum | solution.py:66
  121.6 0.6 subtract_reduce_fusion
  122.3 20.4 %fusion.9 = (f32[1024]{0:T(1024)S(1)}, bf16[1024,256]{0,1:T(8,128)(2,1)S(1)}) fusion(f32[1024,256]{0,1:T(8,128)S(1)} %copy-done.3, f32[1024]{0:T(1024)S(1)} %add_rsqrt_fusion.1, bf16[8192,256]{0,1:T(8,128)(2,1)} %all-gather.3.cloned.1.call-done, f32[1024,8192]{1,0:T(8,128)} %get-tuple-element.27, f32[1024]{0:T(1024)S(1)} %broadcast_multiply_fusion.1, ...), kind=kOutput, calls=%fused_computation.26 | convolution fusion | flops 4363385856 | bytes 39346176 | tf_op jit(solution)/shard_map/dot_general | solution.py:72
  142.6 1.0 fusion.11
  143.6 4.4 fusion.5
  148.1 0.6 broadcast_in_dim.14
  148.7 3.3 all-to-all-start
  152.0 0.0 all-reduce.5.cloned.1.call-start
  152.1 2.9 convolution_convert_fusion.3
  154.9 0.0 all-reduce.5.cloned.1.call-update
  155.0 0.0 all-reduce.9.cloned.1.call-start
  155.0 4.4 all-gather.5.cloned.1.call-done
  159.4 14.2 %multiply_convert_fusion.5.clone.4 = bf16[8192,1024]{1,0:T(8,128)(2,1)S(1)} fusion(f32[8192]{0:T(1024)S(1)} %broadcast_multiply_fusion, s32[1024]{0:T(1024)S(1)} %iota_add_fusion, f32[8192]{0:T(1024)S(1)} %bitcast.31, f32[8192]{0:T(1024)S(1)} %convert_element_type.108, s32[8192]{0:T(1024)S(1)} %bitcast.30, ...), kind=kOutput, calls=%fused_computation.clone.clone.clone.clone.clone.clone.1 | convolution fusion | flops 4362600448 | bytes 22159360 | tf_op jit(solution)/shard_map/ue,ie->ui/dot_general | solution.py:113
  173.6 4.7 fusion.12
  178.3 0.2 fusion.14
  178.6 0.8 copy-done.7
  179.3 1.2 convolution_convert_fusion.2
  180.5 4.4 fusion.6
  184.9 0.0 all-reduce.9.cloned.1.call-update
  184.9 0.0 all-reduce.7.cloned.1.call-start
  185.0 95.5 %all-reduce.5.cloned.1.call-done = bf16[1024,512]{0,1:T(8,128)(2,1)} async-done(((bf16[1024,512]{0,1:T(8,128)(2,1)}), bf16[1024,512]{0,1:T(8,128)(2,1)}) %all-reduce.5.cloned.1.call-update) | async-done | bytes 1048592 | tf_op jit(solution)/shard_map/psum | solution.py:10
  280.4 0.0 all-reduce.7.cloned.1.call-update
  280.5 67.8 %psum.42 = bf16[]{:T(256)} all-reduce(bf16[]{:T(256)} %get-tuple-element.20), channel_id=1, replica_groups=mesh['row'=8,'col'=16] {'row','col'}, use_global_device_ids=true, to_apply=%region_6.7 | all-reduce | flops 1 | bytes 4 | tf_op jit(solution)/shard_map/psum | solution.py:146
  349.0 88.4 %all-reduce.9.cloned.1.call-done = (bf16[1024,512]{0,1:T(8,128)(2,1)}, bf16[512,256]{1,0:T(8,128)(2,1)}, bf16[512,256]{1,0:T(8,128)(2,1)}) async-done(((bf16[1024,512]{0,1:T(8,128)(2,1)}, bf16[512,256]{1,0:T(8,128)(2,1)}, bf16[512,256]{1,0:T(8,128)(2,1)}), (bf16[1024,512]{0,1:T(8,128)(2,1)}, bf16[512,256]{1,0:T(8,128)(2,1)}, bf16[512,256]{1,0:T(8,128)(2,1)})) %all-reduce.9.cloned.1.call-update) | async-done | bytes 1572880 | tf_op jit(solution)/shard_map/psum | solution.py:144
  437.4 1.8 convert_element_type.107
  439.2 2.6 copy.16
  441.7 1.8 convert_element_type.119
  443.5 77.3 %all-reduce.7.cloned.1.call-done = bf16[1024,512]{0,1:T(8,128)(2,1)} async-done(((bf16[1024,512]{0,1:T(8,128)(2,1)}), bf16[1024,512]{0,1:T(8,128)(2,1)}) %all-reduce.7.cloned.1.call-update) | async-done | bytes 1048592 | tf_op jit(solution)/shard_map/psum | solution.py:11
  520.8 2.6 copy.15
  (35 shorter events, 0.1 us)
Async XLA Ops:
  7.2 15.1 %copy-start = (bf16[1024,1024]{1,0:T(8,128)(2,1)S(1)}, bf16[1024,1024]{1,0:T(8,128)(2,1)}, u32[]{:S(2)}) copy-start(bf16[1024,1024]{1,0:T(8,128)(2,1)} %param.8) | copy-start | bytes 6291460
  7.2 4.7 copy-start.9
  7.2 80.0 %all-gather.3.cloned.1.call-start = ((), (), s32[]{:S(2)}) async-start(), calls=%async_computation.2 | async-start | bytes 4718592 | tf_op jit(solution)/shard_map/all_gather | solution.py:96
  10.5 1.3 copy-start.4
  11.8 1.4 copy-start.12
  13.9 134.1 %all-to-all-start.1 = ((s32[8,1,1024]{2,1,0:T(1,128)}), s32[8,1,1024]{2,1,0:T(1,128)S(1)}, u32[]{:S(2)}, u32[]{:S(2)}) async-start(s32[8,1,1024]{2,1,0:T(1,128)} %broadcast_in_dim.15), calls=%async_computation.1 | async-start | bytes 65536 | tf_op jit(solution)/shard_map/all_to_all | solution.py:22
  22.2 3.9 copy-start.8
  22.2 137.2 %all-gather.5.cloned.1.call-start = ((), (), s32[]{:S(2)}) async-start(), calls=%async_computation.5 | async-start | bytes 4718592 | tf_op jit(solution)/shard_map/all_gather | solution.py:105
  24.8 1.3 copy-start.6
  26.1 2.4 copy-start.11
  26.6 1.0 copy-start.2
  103.2 19.0 %copy-start.3 = (f32[1024,256]{0,1:T(8,128)S(1)}, f32[1024,256]{0,1:T(8,128)}, u32[]{:S(2)}) copy-start(f32[1024,256]{0,1:T(8,128)} %copy-done.2) | copy-start | bytes 3145732
  148.7 10.7 %all-to-all-start = ((f32[8,1,1024]{2,1,0:T(1,128)}), f32[8,1,1024]{2,1,0:T(1,128)S(1)}, u32[]{:S(2)}, u32[]{:S(2)}) async-start(f32[8,1,1024]{2,1,0:T(1,128)} %broadcast_in_dim.14), calls=%async_computation | async-start | bytes 65536 | tf_op jit(solution)/shard_map/all_to_all | solution.py:22
  152.0 128.4 %all-reduce.5.cloned.1.call-start = ((), (), s32[]{:S(2)}) async-start(), calls=%async_computation.3 | async-start | bytes 2097152 | tf_op jit(solution)/shard_map/psum | solution.py:10
  155.0 282.4 %all-reduce.9.cloned.1.call-start = ((), (), s32[]{:S(2)}) async-start(), calls=%async_computation.6 | async-start | bytes 3145728 | tf_op jit(solution)/shard_map/psum | solution.py:144
  159.4 14.2 %copy-start.13 = (bf16[8192,256]{0,1:T(8,128)(2,1)S(1)}, bf16[8192,256]{0,1:T(8,128)(2,1)}, u32[]{:S(2)}) copy-start(bf16[8192,256]{0,1:T(8,128)(2,1)} %all-gather.5.cloned.1.call-done) | copy-start | bytes 12582916
  173.6 5.7 %copy-start.5 = (f32[1024,512]{1,0:T(8,128)S(1)}, f32[1024,512]{1,0:T(8,128)}, u32[]{:S(2)}) copy-start(f32[1024,512]{1,0:T(8,128)} %copy-done.4) | copy-start | bytes 6291460
  178.3 2.2 copy-start.10
  178.5 0.8 copy-start.7
  184.9 335.9 %all-reduce.7.cloned.1.call-start = ((), (), s32[]{:S(2)}) async-start(), calls=%async_computation.4 | async-start | bytes 2097152 | tf_op jit(solution)/shard_map/psum | solution.py:11
  280.5 242.9 %copy-start.1 = (bf16[1024,1024]{1,0:T(8,128)(2,1)S(1)}, bf16[1024,1024]{1,0:T(8,128)(2,1)}, u32[]{:S(2)}) copy-start(bf16[1024,1024]{1,0:T(8,128)(2,1)} %param.8) | copy-start | bytes 6291460
Sparse Core Ops, SparseCore 0:
  13.4 73.7 all-gather.2
  90.1 69.2 all-gather.4
  161.9 118.5 all-reduce.4
  285.9 151.4 all-reduce.8
  439.7 80.9 all-reduce.6
